TPU v7x, 32 devices: a whole 2x2x4 slice. The times are simulated.
32 devices in a mesh: blk: 8 (over z, x), rows: 4 (over y, core).
Axes of the slice: x: 2, y: 2, z: 4, core: 2. Of those that a mesh axis runs over, the one named last changes fastest.
Arguments:
- columns: float32 [512, 16384], P('blk', 'rows'), may hold values from -100 to 100
- plan: int32 [3, 16], replicated, may hold values from 0 to 15, as said below
Outputs:
- swept: float32 [512, 16384], P('blk', 'rows')
- off_ratio: float32 [3], replicated
Inputs may be any that keep to these rules, and one draw needn't show every extreme that they name: `plan`: row s is a permutation of the 16 positions (position k is slot k % 2 of blk index k // 2). In each row there are a slot t and a number m of 1 to 7 such that the block in slot t of every blk index i goes to slot t of blk index (i + m) modulo 16 / 2, and every other block stays where it is.
All inputs are finite; a program needn't handle non-finite values. Where the computation divides by a largest or mean magnitude, that divisor is 1e-20 or more.
Results may differ from a plain program's by a relative error of at most 0.00011.
Values sent between devices are 32-bit elements; how exact they have to be, the bound alone decides.
No kernel may reach another device: no remote copies, remote signals or barrier semaphores. Data moves between devices by JAX's collectives and lax.ppermute only.
A program may use at most 64 MiB of HBM per device.

v0:
```python
from functools import partial
import jax
import jax.numpy as jnp
from jax import lax
from jax.sharding import PartitionSpec as P

STEPS = 3
EIG_ITERS = 3
NS_ITERS = 8
PRECISE = lax.Precision.HIGHEST


def shifted(value, axis, steps):
    count = lax.axis_size(axis)
    pairs = [(source, (source + steps) % count) for source in range(count)]
    return lax.ppermute(value, axis, pairs)


def matmul(left, right):
    return jnp.matmul(left, right, precision=PRECISE, preferred_element_type=jnp.float32)


def orthonormal(matrix):
    lengths = jnp.sqrt(jnp.sum(matrix * matrix, axis=0, keepdims=True))
    normed = matrix / lengths
    inner = matmul(normed.T, normed)
    bound = jnp.max(jnp.sum(jnp.abs(inner), axis=1))
    normed = normed / jnp.sqrt(bound)
    for turn_index in range(NS_ITERS):
        normed = 1.5 * normed - 0.5 * matmul(normed, matmul(normed.T, normed))
    return normed


def pair_rotation(gram_sum):
    rotation = jnp.eye(gram_sum.shape[0], dtype=gram_sum.dtype)
    for turn_index in range(EIG_ITERS):
        rotation = orthonormal(matmul(gram_sum, rotation))
    return rotation


def move_by(values, distance):
    return shifted(values, "blk", distance)


def local(columns, plan):
    block_width = columns.shape[0] // 2
    cycle_size = lax.axis_size("blk")
    eye_mask = jnp.eye(2 * block_width, dtype=bool)
    current = columns
    off_list = []
    diag_list = []
    for step_index in range(STEPS):
        partial_gram = matmul(current, current.T)
        gram_sum = lax.psum(partial_gram, "rows")
        off_part = jnp.where(eye_mask, 0.0, gram_sum)
        diag_part = jnp.where(eye_mask, gram_sum, 0.0)
        off_local = jnp.sum(off_part * off_part)
        diag_local = jnp.sum(diag_part * diag_part)
        off_total, diag_total = lax.psum((off_local, diag_local), "blk")
        off_list.append(off_total)
        diag_list.append(diag_total)
        rotation = pair_rotation(gram_sum)
        rotated = matmul(rotation.T, current)
        first_dest = plan[step_index, 0]
        second_dest = plan[step_index, 1]
        partner_step = jnp.maximum(first_dest // 2, second_dest // 2)
        leaving_high = second_dest != 1
        moving = jnp.where(leaving_high, rotated[block_width:], rotated[:block_width])
        staying = jnp.where(leaving_high, rotated[:block_width], rotated[block_width:])
        branches = [partial(move_by, distance=distance) for distance in range(1, cycle_size)]
        moving = lax.switch(partner_step - 1, branches, moving)
        current = jnp.where(
            leaving_high,
            jnp.concatenate([staying, moving], axis=0),
            jnp.concatenate([moving, staying], axis=0),
        )
    off_sums = jnp.stack(off_list)
    diag_sums = jnp.stack(diag_list)
    return (current, jnp.sqrt(off_sums) / jnp.sqrt(diag_sums))


def solution(mesh):
    return jax.shard_map(
        local,
        mesh=mesh,
        in_specs=(P("blk", "rows"), P()),
        out_specs=(P("blk", "rows"), P()),
        check_vma=False,
    )
```

profile of v0, /device:TPU:0, one launch (start us, length us, event | category | flops | bytes accessed | tf_op | source)
XLA Modules:
  0.0 189.1 jit_solution(8808458993383925959)
XLA Ops:
  0.6 1.6 fusion.124
  19.2 1.0 fusion.125
  20.2 12.9 %psum.63 = f32[64,64]{1,0:T(8,128)S(1)} all-reduce(f32[64,64]{1,0:T(8,128)S(1)} %fusion.125), channel_id=1, replica_groups=mesh['blk'=8,'rows'=4] {'rows'}, use_global_device_ids=true, to_apply=%region_0.0 | all-reduce | flops 4096 | bytes 32768 | tf_op jit(solution)/shard_map/psum | solution.py:54
  33.1 0.7 multiply_reduce_fusion.2
  49.1 1.0 fusion.147
  50.2 13.9 %conditional.3 = (f32[32,4096]{1,0:T(8,128)}) conditional(s32[]{:T(128)} %clamp.9, f32[32,4096]{1,0:T(8,128)S(1)} %get-tuple-element.64, f32[32,4096]{1,0:T(8,128)S(1)} %get-tuple-element.64, f32[32,4096]{1,0:T(8,128)S(1)} %get-tuple-element.64, f32[32,4096]{1,0:T(8,128)S(1)} %get-tuple-element.64, ...), branch_computations={%region_10.11_spmd, %region_11.12_spmd, %region_12.13_spmd, %regio... | conditional | bytes 2097200 | solution.py:71
  50.2 3.7 %collective-permute-start.5 = (f32[32,4096]{1,0:T(8,128)S(1)}, f32[32,4096]{1,0:T(8,128)}, u32[]{:S(2)}, u32[]{:S(2)}) collective-permute-start(f32[32,4096]{1,0:T(8,128)S(1)} %param.5), channel_id=1, source_target_pairs={{0,24},{4,28},{8,0},{12,4},{16,8},{20,12},{24,16},{28,20},{1,25},{... | collective-permute-start | bytes 1572872 | tf_op jit(solution)/shard_map/cond/branch_5_fun/ppermute | solution.py:16
  53.9 10.2 %collective-permute-done.5 = f32[32,4096]{1,0:T(8,128)} collective-permute-done((f32[32,4096]{1,0:T(8,128)S(1)}, f32[32,4096]{1,0:T(8,128)}, u32[]{:S(2)}, u32[]{:S(2)}) %collective-permute-start.5) | collective-permute-done | bytes 524320 | tf_op jit(solution)/shard_map/cond/branch_5_fun/ppermute | solution.py:16
  64.0 2.7 %fusion.84 = f32[64,64]{1,0:T(8,128)S(1)} fusion(f32[32,4096]{1,0:T(8,128)} %get-tuple-element.89, f32[32,4096]{1,0:T(8,128)S(1)} %get-tuple-element.63, pred[]{:T(512)S(6)} %ne.49), kind=kOutput, calls=%fused_computation.168 | convolution fusion | flops 202113024 | bytes 1064961 | tf_op jit(solution)/shard_map/dot_general | solution.py:20
  66.8 10.7 %psum.64 = f32[64,64]{1,0:T(8,128)S(1)} all-reduce(f32[64,64]{1,0:T(8,128)S(1)} %fusion.84), channel_id=1, replica_groups=mesh['blk'=8,'rows'=4] {'rows'}, use_global_device_ids=true, to_apply=%region_17.18 | all-reduce | flops 4096 | bytes 32768 | tf_op jit(solution)/shard_map/psum | solution.py:54
  77.5 0.7 multiply_reduce_fusion.1
  93.4 2.3 %fusion.83 = f32[64,4096]{1,0:T(8,128)S(1)} fusion(f32[64,64]{1,0:T(8,128)S(1)} %fusion.24, f32[32,4096]{1,0:T(8,128)} %get-tuple-element.89, f32[32,4096]{1,0:T(8,128)S(1)} %get-tuple-element.63, pred[]{:T(512)S(6)} %ne.49), kind=kOutput, calls=%fused_computation.167 | convolution fusion | flops 202113024 | bytes 2113537 | tf_op jit(solution)/shard_map/dot_general | solution.py:20
  95.8 27.1 %conditional.4 = (f32[32,4096]{1,0:T(8,128)}) conditional(s32[]{:T(128)} %clamp.10, f32[32,4096]{1,0:T(8,128)S(1)} %get-tuple-element.62, f32[32,4096]{1,0:T(8,128)S(1)} %get-tuple-element.62, f32[32,4096]{1,0:T(8,128)S(1)} %get-tuple-element.62, f32[32,4096]{1,0:T(8,128)S(1)} %get-tuple-element.62, ...), branch_computations={%region_27.28_spmd, %region_28.29_spmd, %region_29.30_spmd, %regio... | conditional | bytes 2097200 | solution.py:71
  95.8 1.5 collective-permute-start.9
  97.4 25.6 %collective-permute-done.9 = f32[32,4096]{1,0:T(8,128)} collective-permute-done((f32[32,4096]{1,0:T(8,128)S(1)}, f32[32,4096]{1,0:T(8,128)}, u32[]{:S(2)}, u32[]{:S(2)}) %collective-permute-start.9) | collective-permute-done | bytes 524320 | tf_op jit(solution)/shard_map/cond/branch_2_fun/ppermute | solution.py:16
  122.9 2.7 %fusion.82 = f32[64,64]{1,0:T(8,128)S(1)} fusion(f32[32,4096]{1,0:T(8,128)} %get-tuple-element.90, f32[32,4096]{1,0:T(8,128)S(1)} %get-tuple-element.61, pred[]{:T(512)S(6)} %ne.48), kind=kOutput, calls=%fused_computation.166 | convolution fusion | flops 202113024 | bytes 1064961 | tf_op jit(solution)/shard_map/dot_general | solution.py:20
  125.7 10.3 %psum.65 = f32[64,64]{1,0:T(8,128)S(1)} all-reduce(f32[64,64]{1,0:T(8,128)S(1)} %fusion.82), channel_id=1, replica_groups=mesh['blk'=8,'rows'=4] {'rows'}, use_global_device_ids=true, to_apply=%region_34.35 | all-reduce | flops 4096 | bytes 32768 | tf_op jit(solution)/shard_map/psum | solution.py:54
  136.6 18.0 %all-reduce = (f32[1]{0:T(128)}, f32[1]{0:T(128)}, f32[1]{0:T(128)}, f32[1]{0:T(128)}, f32[1]{0:T(128)}, /*index=5*/f32[1]{0:T(128)}) all-reduce(f32[1]{0:T(128)} %bitcast.8, f32[1]{0:T(128)} %bitcast.7, f32[1]{0:T(128)} %bitcast.6, f32[1]{0:T(128)} %bitcast.11, f32[1]{0:T(128)} %bitcast.10, ...), channel_id=1, replica_groups=mesh['blk'=8,'rows'=4] {'blk'}, use_global_device_ids=true, to_apply=%region_56.57 | all-reduce | flops 6 | bytes 48 | tf_op jit(solution)/shard_map/psum | solution.py:59
  154.6 4.3 %fusion.119 = f32[3]{0:T(128)} fusion(f32[1]{0:T(128)} %get-tuple-element.53, f32[1]{0:T(128)} %get-tuple-element.54, f32[1]{0:T(128)} %get-tuple-element.55, f32[1]{0:T(128)} %get-tuple-element.56, f32[1]{0:T(128)} %get-tuple-element.57, f32[1]{0:T(128)} %get-tuple-element.58), kind=kLoop, calls=%fused_computation.235 | loop fusion | flops 15 | bytes 36 | tf_op jit(solution)/shard_map/div | solution.py:79
  174.2 2.3 %fusion.81 = f32[64,4096]{1,0:T(8,128)S(1)} fusion(f32[64,64]{1,0:T(8,128)S(1)} %fusion, f32[32,4096]{1,0:T(8,128)} %get-tuple-element.90, f32[32,4096]{1,0:T(8,128)S(1)} %get-tuple-element.61, pred[]{:T(512)S(6)} %ne.48), kind=kOutput, calls=%fused_computation.165 | convolution fusion | flops 202113024 | bytes 2113537 | tf_op jit(solution)/shard_map/dot_general | solution.py:20
  176.6 10.3 %conditional.5 = (f32[32,4096]{1,0:T(8,128)}) conditional(s32[]{:T(128)} %clamp.11, f32[32,4096]{1,0:T(8,128)S(1)} %get-tuple-element.60, f32[32,4096]{1,0:T(8,128)S(1)} %get-tuple-element.60, f32[32,4096]{1,0:T(8,128)S(1)} %get-tuple-element.60, f32[32,4096]{1,0:T(8,128)S(1)} %get-tuple-element.60, ...), branch_computations={%region_44.45_spmd, %region_45.46_spmd, %region_46.47_spmd, %regio... | conditional | bytes 2097200 | solution.py:71
  176.6 2.1 %collective-permute-start.20 = (f32[32,4096]{1,0:T(8,128)S(1)}, f32[32,4096]{1,0:T(8,128)}, u32[]{:S(2)}, u32[]{:S(2)}) collective-permute-start(f32[32,4096]{1,0:T(8,128)S(1)} %param.20), channel_id=1, source_target_pairs={{0,28},{4,0},{8,4},{12,8},{16,12},{20,16},{24,20},{28,24},{1,29},{... | collective-permute-start | bytes 1572872 | tf_op jit(solution)/shard_map/cond/branch_6_fun/ppermute | solution.py:16
  178.7 8.2 %collective-permute-done.20 = f32[32,4096]{1,0:T(8,128)} collective-permute-done((f32[32,4096]{1,0:T(8,128)S(1)}, f32[32,4096]{1,0:T(8,128)}, u32[]{:S(2)}, u32[]{:S(2)}) %collective-permute-start.20) | collective-permute-done | bytes 524320 | tf_op jit(solution)/shard_map/cond/branch_6_fun/ppermute | solution.py:16
  186.8 2.3 %maximum_select_fusion.2 = f32[64,4096]{1,0:T(8,128)} fusion(f32[32,4096]{1,0:T(8,128)} %get-tuple-element.91, f32[32,4096]{1,0:T(8,128)S(1)} %get-tuple-element.59, pred[]{:T(512)S(6)} %ne.47), kind=kLoop, calls=%fused_computation.164 | loop fusion | flops 786432 | bytes 2097153 | tf_op jit(solution)/shard_map/jit(_where)/select_n | solution.py:72
  (195 shorter events, 39.1 us)
Async XLA Ops:
  0.6 18.6 %copy-start = (f32[64,4096]{1,0:T(8,128)S(1)}, f32[64,4096]{1,0:T(8,128)}, u32[]{:S(2)}) copy-start(f32[64,4096]{1,0:T(8,128)} %param.23) | copy-start | bytes 3145732
  50.2 13.8 %collective-permute-start.5 = (f32[32,4096]{1,0:T(8,128)S(1)}, f32[32,4096]{1,0:T(8,128)}, u32[]{:S(2)}, u32[]{:S(2)}) collective-permute-start(f32[32,4096]{1,0:T(8,128)S(1)} %param.5), channel_id=1, source_target_pairs={{0,24},{4,28},{8,0},{12,4},{16,8},{20,12},{24,16},{28,20},{1,25},{... | collective-permute-start | bytes 1572872 | tf_op jit(solution)/shard_map/cond/branch_5_fun/ppermute | solution.py:16
  95.8 27.1 %collective-permute-start.9 = (f32[32,4096]{1,0:T(8,128)S(1)}, f32[32,4096]{1,0:T(8,128)}, u32[]{:S(2)}, u32[]{:S(2)}) collective-permute-start(f32[32,4096]{1,0:T(8,128)S(1)} %param.9), channel_id=1, source_target_pairs={{0,12},{4,16},{8,20},{12,24},{16,28},{20,0},{24,4},{28,8},{1,13},{... | collective-permute-start | bytes 1572872 | tf_op jit(solution)/shard_map/cond/branch_2_fun/ppermute | solution.py:16
  176.6 10.2 %collective-permute-start.20 = (f32[32,4096]{1,0:T(8,128)S(1)}, f32[32,4096]{1,0:T(8,128)}, u32[]{:S(2)}, u32[]{:S(2)}) collective-permute-start(f32[32,4096]{1,0:T(8,128)S(1)} %param.20), channel_id=1, source_target_pairs={{0,28},{4,0},{8,4},{12,8},{16,12},{20,16},{24,20},{28,24},{1,29},{... | collective-permute-start | bytes 1572872 | tf_op jit(solution)/shard_map/cond/branch_6_fun/ppermute | solution.py:16
where the time goes:
time: 190 us; the launch traced here: 189 us
  blocking collectives  51.9 us (27%)
  matrix products  44.7 us (24%)
  waiting for transfers between devices  43.9 us (23%)
  between operations  25.2 us (13%)
  other arithmetic  14.3 us (8%)
  starting transfers between devices  7.26 us (4%)
    dot_general x168, matrix products, matmul(): jnp.matmul(left, right, precision=PRECISE, preferred_element_type=jnp.flo...  44.7 us
    ppermute x3, waiting for transfers between devices, shifted(): return lax.ppermute(value, axis, pairs)  43.9 us
    psum x3, blocking collectives, local(): gram_sum = lax.psum(partial_gram, 'rows')  33.9 us
    psum x1, blocking collectives, local(): off_total, diag_total = lax.psum((off_local, diag_local), 'blk')  18 us
    ppermute x3, starting transfers between devices, shifted(): return lax.ppermute(value, axis, pairs)  7.26 us
    reduce_max x9, other arithmetic, orthonormal(): bound = jnp.max(jnp.sum(jnp.abs(inner), axis=1))  5.47 us
    div x1, other arithmetic, local(): return (current, jnp.sqrt(off_sums) / jnp.sqrt(diag_sums))  4.33 us
  transfers between devices with their start and end apart: 3, of which 3 were waited for; matrix products, arithmetic and copies ran while one was open for 0% of the time, Pallas kernels for 0%

commit v1 on v0

--- a/solution.py
+++ b/solution.py
@@ -51,7 +51,10 @@
     diag_list = []
     for step_index in range(STEPS):
         partial_gram = matmul(current, current.T)
-        gram_sum = lax.psum(partial_gram, "rows")
+        count_2, gram_sum = (lax.axis_size("rows"), partial_gram)
+        for stride in [1 << k for k in range(count_2.bit_length() - 1)]:
+            swap = [(i, i ^ stride) for i in range(count_2)]
+            gram_sum = gram_sum + lax.ppermute(gram_sum, "rows", swap)
         off_part = jnp.where(eye_mask, 0.0, gram_sum)
         diag_part = jnp.where(eye_mask, gram_sum, 0.0)
         off_local = jnp.sum(off_part * off_part)

time: 190 us -> 172 us (0.905)
  blocking collectives: 51.9 us -> 20.8 us
  waiting for transfers between devices: 43.9 us -> 53.6 us
  starting transfers between devices: 7.26 us -> 10.9 us
    psum x3 -> x0, blocking collectives: 33.9 us -> none  [local(): gram_sum = lax.psum(partial_gram, 'rows')]
    ppermute x3, waiting for transfers between devices: 43.9 us -> 50.3 us  [shifted(): return lax.ppermute(value, axis, pairs)]
    ppermute x0 -> x6, starting transfers between devices: none -> 5.64 us  [local(): gram_sum = gram_sum + lax.ppermute(gram_sum, 'rows', swap)]
    ppermute x0 -> x6, waiting for transfers between devices: none -> 3.26 us  [local(): gram_sum = gram_sum + lax.ppermute(gram_sum, 'rows', swap)]
    psum x1, blocking collectives: 18 us -> 20.8 us  [local(): off_total, diag_total = lax.psum((off_local, diag_local), 'blk')]
    ppermute x3, starting transfers between devices: 7.26 us -> 5.26 us  [shifted(): return lax.ppermute(value, axis, pairs)]
  transfers between devices with their start and end apart: 3 -> 9, of which waited for: 3 -> 6; matrix products, arithmetic and copies ran while one was open for 0% -> 0% of each run, Pallas kernels for 0% -> 0%
where the time goes in v1:
time: 172 us
  waiting for transfers between devices  53.6 us (31%)
  matrix products  44.7 us (26%)
  between operations  25.3 us (15%)
  blocking collectives  20.8 us (12%)
  other arithmetic  14.4 us (8%)
  starting transfers between devices  10.9 us (6%)
  local copies, waits for them, and re-layouts  1.95 us (1%)
    ppermute x3, waiting for transfers between devices, shifted(): return lax.ppermute(value, axis, pairs)  50.3 us
    dot_general x168, matrix products, matmul(): jnp.matmul(left, right, precision=PRECISE, preferred_element_type=jnp.flo...  44.7 us
    psum x1, blocking collectives, local(): off_total, diag_total = lax.psum((off_local, diag_local), 'blk')  20.8 us
    ppermute x6, starting transfers between devices, local(): gram_sum = gram_sum + lax.ppermute(gram_sum, 'rows', swap)  5.64 us
    reduce_max x9, other arithmetic, orthonormal(): bound = jnp.max(jnp.sum(jnp.abs(inner), axis=1))  5.47 us
    ppermute x3, starting transfers between devices, shifted(): return lax.ppermute(value, axis, pairs)  5.26 us
    div x1, other arithmetic, local(): return (current, jnp.sqrt(off_sums) / jnp.sqrt(diag_sums))  4.33 us
  transfers between devices with their start and end apart: 9, of which 6 were waited for; matrix products, arithmetic and copies ran while one was open for 0% of the time, Pallas kernels for 0%

profile of v1, /device:TPU:0, one launch (start us, length us, event | category | flops | bytes accessed | tf_op | source)
XLA Modules:
  0.0 171.7 jit_solution(522474329371897323)
XLA Ops:
  0.6 1.2 copy-done
  1.9 1.0 fusion.116
  3.4 0.9 collective-permute-done.21
  4.3 2.9 %collective-permute-start.22 = (f32[64,64]{1,0:T(8,128)S(1)}, f32[64,64]{1,0:T(8,128)S(1)}, u32[]{:S(2)}, u32[]{:S(2)}) collective-permute-start(f32[64,64]{1,0:T(8,128)S(1)} %add.39), channel_id=1, source_target_pairs={{0,2},{1,3},{2,0},{3,1},{4,6},{5,7},{6,4},{7,5},{8,10},{9,11},{10,... | collective-permute-start | bytes 49160 | tf_op jit(solution)/shard_map/ppermute | solution.py:57
  29.7 1.0 fusion.138
  30.8 14.9 %conditional.3 = (f32[32,4096]{1,0:T(8,128)}) conditional(s32[]{:T(128)} %clamp.9, f32[32,4096]{1,0:T(8,128)S(1)} %get-tuple-element.67, f32[32,4096]{1,0:T(8,128)S(1)} %get-tuple-element.67, f32[32,4096]{1,0:T(8,128)S(1)} %get-tuple-element.67, f32[32,4096]{1,0:T(8,128)S(1)} %get-tuple-element.67, ...), branch_computations={%region_9.10_spmd, %region_10.11_spmd, %region_11.12_spmd, %region... | conditional | bytes 2097200 | solution.py:74
  30.8 3.7 %collective-permute-start.5 = (f32[32,4096]{1,0:T(8,128)S(1)}, f32[32,4096]{1,0:T(8,128)}, u32[]{:S(2)}, u32[]{:S(2)}) collective-permute-start(f32[32,4096]{1,0:T(8,128)S(1)} %param.5), channel_id=1, source_target_pairs={{0,24},{4,28},{8,0},{12,4},{16,8},{20,12},{24,16},{28,20},{1,25},{... | collective-permute-start | bytes 1572872 | tf_op jit(solution)/shard_map/cond/branch_5_fun/ppermute | solution.py:16
  34.5 11.2 %collective-permute-done.5 = f32[32,4096]{1,0:T(8,128)} collective-permute-done((f32[32,4096]{1,0:T(8,128)S(1)}, f32[32,4096]{1,0:T(8,128)}, u32[]{:S(2)}, u32[]{:S(2)}) %collective-permute-start.5) | collective-permute-done | bytes 524320 | tf_op jit(solution)/shard_map/cond/branch_5_fun/ppermute | solution.py:16
  45.7 2.7 %fusion.75 = f32[64,64]{1,0:T(8,128)S(1)} fusion(f32[32,4096]{1,0:T(8,128)} %get-tuple-element.92, f32[32,4096]{1,0:T(8,128)S(1)} %get-tuple-element.66, pred[]{:T(512)S(6)} %ne.49), kind=kOutput, calls=%fused_computation.159 | convolution fusion | flops 202113024 | bytes 1064961 | tf_op jit(solution)/shard_map/dot_general | solution.py:20
  48.5 1.2 collective-permute-done.23
  49.7 0.9 collective-permute-start.24
  72.2 2.3 %fusion.74 = f32[64,4096]{1,0:T(8,128)S(1)} fusion(f32[64,64]{1,0:T(8,128)S(1)} %fusion.21, f32[32,4096]{1,0:T(8,128)} %get-tuple-element.92, f32[32,4096]{1,0:T(8,128)S(1)} %get-tuple-element.66, pred[]{:T(512)S(6)} %ne.49), kind=kOutput, calls=%fused_computation.158 | convolution fusion | flops 202113024 | bytes 2113537 | tf_op jit(solution)/shard_map/dot_general | solution.py:20
  74.5 26.9 %conditional.4 = (f32[32,4096]{1,0:T(8,128)}) conditional(s32[]{:T(128)} %clamp.10, f32[32,4096]{1,0:T(8,128)S(1)} %get-tuple-element.65, f32[32,4096]{1,0:T(8,128)S(1)} %get-tuple-element.65, f32[32,4096]{1,0:T(8,128)S(1)} %get-tuple-element.65, f32[32,4096]{1,0:T(8,128)S(1)} %get-tuple-element.65, ...), branch_computations={%region_25.26_spmd, %region_26.27_spmd, %region_27.28_spmd, %regio... | conditional | bytes 2097200 | solution.py:74
  74.6 1.5 collective-permute-start.9
  76.1 25.4 %collective-permute-done.9 = f32[32,4096]{1,0:T(8,128)} collective-permute-done((f32[32,4096]{1,0:T(8,128)S(1)}, f32[32,4096]{1,0:T(8,128)}, u32[]{:S(2)}, u32[]{:S(2)}) %collective-permute-start.9) | collective-permute-done | bytes 524320 | tf_op jit(solution)/shard_map/cond/branch_2_fun/ppermute | solution.py:16
  101.5 2.7 %fusion.73 = f32[64,64]{1,0:T(8,128)S(1)} fusion(f32[32,4096]{1,0:T(8,128)} %get-tuple-element.93, f32[32,4096]{1,0:T(8,128)S(1)} %get-tuple-element.64, pred[]{:T(512)S(6)} %ne.48), kind=kOutput, calls=%fused_computation.157 | convolution fusion | flops 202113024 | bytes 1064961 | tf_op jit(solution)/shard_map/dot_general | solution.py:20
  104.3 1.2 collective-permute-done.25
  105.5 1.1 collective-permute-start.26
  128.0 2.3 %fusion.72 = f32[64,4096]{1,0:T(8,128)S(1)} fusion(f32[64,64]{1,0:T(8,128)S(1)} %fusion, f32[32,4096]{1,0:T(8,128)} %get-tuple-element.93, f32[32,4096]{1,0:T(8,128)S(1)} %get-tuple-element.64, pred[]{:T(512)S(6)} %ne.48), kind=kOutput, calls=%fused_computation.156 | convolution fusion | flops 202113024 | bytes 2113537 | tf_op jit(solution)/shard_map/dot_general | solution.py:20
  130.4 13.9 %conditional.5 = (f32[32,4096]{1,0:T(8,128)}) conditional(s32[]{:T(128)} %clamp.11, f32[32,4096]{1,0:T(8,128)S(1)} %get-tuple-element.63, f32[32,4096]{1,0:T(8,128)S(1)} %get-tuple-element.63, f32[32,4096]{1,0:T(8,128)S(1)} %get-tuple-element.63, f32[32,4096]{1,0:T(8,128)S(1)} %get-tuple-element.63, ...), branch_computations={%region_41.42_spmd, %region_42.43_spmd, %region_43.44_spmd, %regio... | conditional | bytes 2097200 | solution.py:74
  130.5 13.8 %collective-permute-done.20 = f32[32,4096]{1,0:T(8,128)} collective-permute-done((f32[32,4096]{1,0:T(8,128)S(1)}, f32[32,4096]{1,0:T(8,128)}, u32[]{:S(2)}, u32[]{:S(2)}) %collective-permute-start.20) | collective-permute-done | bytes 524320 | tf_op jit(solution)/shard_map/cond/branch_6_fun/ppermute | solution.py:16
  144.3 2.3 %maximum_select_fusion.2 = f32[64,4096]{1,0:T(8,128)} fusion(f32[32,4096]{1,0:T(8,128)} %get-tuple-element.94, f32[32,4096]{1,0:T(8,128)S(1)} %get-tuple-element.62, pred[]{:T(512)S(6)} %ne.47), kind=kLoop, calls=%fused_computation.155 | loop fusion | flops 786432 | bytes 2097153 | tf_op jit(solution)/shard_map/jit(_where)/select_n | solution.py:75
  146.6 20.8 %all-reduce = (f32[1]{0:T(128)}, f32[1]{0:T(128)}, f32[1]{0:T(128)}, f32[1]{0:T(128)}, f32[1]{0:T(128)}, /*index=5*/f32[1]{0:T(128)}) all-reduce(f32[1]{0:T(128)} %bitcast.8, f32[1]{0:T(128)} %bitcast.7, f32[1]{0:T(128)} %bitcast.6, f32[1]{0:T(128)} %bitcast.11, f32[1]{0:T(128)} %bitcast.10, ...), channel_id=1, replica_groups=mesh['blk'=8,'rows'=4] {'blk'}, use_global_device_ids=true, to_apply=%region_53.54 | all-reduce | flops 6 | bytes 48 | tf_op jit(solution)/shard_map/psum | solution.py:62
  167.4 4.3 %fusion.110 = f32[3]{0:T(128)} fusion(f32[1]{0:T(128)} %get-tuple-element.53, f32[1]{0:T(128)} %get-tuple-element.54, f32[1]{0:T(128)} %get-tuple-element.55, f32[1]{0:T(128)} %get-tuple-element.56, f32[1]{0:T(128)} %get-tuple-element.57, f32[1]{0:T(128)} %get-tuple-element.58), kind=kLoop, calls=%fused_computation.235 | loop fusion | flops 15 | bytes 36 | tf_op jit(solution)/shard_map/div | solution.py:82
  (209 shorter events, 42.0 us)
Async XLA Ops:
  0.6 1.2 copy-start
  2.8 1.4 collective-permute-start.21
  4.3 2.9 %copy-start.1 = (s32[3,16]{1,0:T(4,128)S(1)}, s32[3,16]{1,0:T(4,128)}, u32[]{:S(2)}) copy-start(s32[3,16]{1,0:T(4,128)} %param.24) | copy-start | bytes 580
  4.3 9.4 %collective-permute-start.22 = (f32[64,64]{1,0:T(8,128)S(1)}, f32[64,64]{1,0:T(8,128)S(1)}, u32[]{:S(2)}, u32[]{:S(2)}) collective-permute-start(f32[64,64]{1,0:T(8,128)S(1)} %add.39), channel_id=1, source_target_pairs={{0,2},{1,3},{2,0},{3,1},{4,6},{5,7},{6,4},{7,5},{8,10},{9,11},{10,... | collective-permute-start | bytes 49160 | tf_op jit(solution)/shard_map/ppermute | solution.py:57
  30.8 14.8 %collective-permute-start.5 = (f32[32,4096]{1,0:T(8,128)S(1)}, f32[32,4096]{1,0:T(8,128)}, u32[]{:S(2)}, u32[]{:S(2)}) collective-permute-start(f32[32,4096]{1,0:T(8,128)S(1)} %param.5), channel_id=1, source_target_pairs={{0,24},{4,28},{8,0},{12,4},{16,8},{20,12},{24,16},{28,20},{1,25},{... | collective-permute-start | bytes 1572872 | tf_op jit(solution)/shard_map/cond/branch_5_fun/ppermute | solution.py:16
  48.4 1.3 collective-permute-start.23
  49.7 6.6 %collective-permute-start.24 = (f32[64,64]{1,0:T(8,128)S(1)}, f32[64,64]{1,0:T(8,128)S(1)}, u32[]{:S(2)}, u32[]{:S(2)}) collective-permute-start(f32[64,64]{1,0:T(8,128)S(1)} %add.41), channel_id=1, source_target_pairs={{0,2},{1,3},{2,0},{3,1},{4,6},{5,7},{6,4},{7,5},{8,10},{9,11},{10,... | collective-permute-start | bytes 49160 | tf_op jit(solution)/shard_map/ppermute | solution.py:57
  74.6 26.9 %collective-permute-start.9 = (f32[32,4096]{1,0:T(8,128)S(1)}, f32[32,4096]{1,0:T(8,128)}, u32[]{:S(2)}, u32[]{:S(2)}) collective-permute-start(f32[32,4096]{1,0:T(8,128)S(1)} %param.9), channel_id=1, source_target_pairs={{0,12},{4,16},{8,20},{12,24},{16,28},{20,0},{24,4},{28,8},{1,13},{... | collective-permute-start | bytes 1572872 | tf_op jit(solution)/shard_map/cond/branch_2_fun/ppermute | solution.py:16
  104.2 1.3 collective-permute-start.25
  105.5 6.6 %collective-permute-start.26 = (f32[64,64]{1,0:T(8,128)S(1)}, f32[64,64]{1,0:T(8,128)S(1)}, u32[]{:S(2)}, u32[]{:S(2)}) collective-permute-start(f32[64,64]{1,0:T(8,128)S(1)} %add.43), channel_id=1, source_target_pairs={{0,2},{1,3},{2,0},{3,1},{4,6},{5,7},{6,4},{7,5},{8,10},{9,11},{10,... | collective-permute-start | bytes 49160 | tf_op jit(solution)/shard_map/ppermute | solution.py:57
  130.4 13.9 %collective-permute-start.20 = (f32[32,4096]{1,0:T(8,128)S(1)}, f32[32,4096]{1,0:T(8,128)}, u32[]{:S(2)}, u32[]{:S(2)}) collective-permute-start(f32[32,4096]{1,0:T(8,128)S(1)} %param.20), channel_id=1, source_target_pairs={{0,28},{4,0},{8,4},{12,8},{16,12},{20,16},{24,20},{28,24},{1,29},{... | collective-permute-start | bytes 1572872 | tf_op jit(solution)/shard_map/cond/branch_6_fun/ppermute | solution.py:16
